TPU v7x, 256 devices: a whole 4x4x8 slice. The times are simulated.
256 devices in a mesh: ra: 16 (over x_hi, y, core), dec: 16 (over z, x_lo).
Axes of the slice: x: 4 (x_hi: 2, x_lo: 2; x = x_hi * 2 + x_lo), y: 4, z: 8, core: 2. Of those that a mesh axis runs over, the one named last changes fastest.
Arguments:
- design: float32 [5, 80, 64, 4096], P(None, None, 'ra', 'dec'), may hold values from -6 to 6
- observed: float32 [80, 64, 4096], P(None, 'ra', 'dec'), may hold values from -6 to 6
- weight: float32 [80, 64, 4096], P(None, 'ra', 'dec'), may hold values from 0.3 to 3
- params: float32 [5, 64, 4096], P(None, 'ra', 'dec'), may hold values from -4 to 4
- offsets: int32 [80, 64, 4096], P(None, 'ra', 'dec'), may hold values from 0 to 8, as said below
- counts: int32 [64, 4096], P('ra', 'dec'), may hold values from 10 to 80, as said below
Outputs:
- new_params: float32 [5, 64, 4096], P(None, 'ra', 'dec')
- reduced_chi: float32 [], replicated
Inputs may be any that keep to these rules, and one draw needn't show every extreme that they name: `offsets`: in the first and the last latitude row of cells no offset steps outside the grid in latitude. `counts`: cells near the middle latitude hold more live observations; the two middle latitude rows hold 80.
All inputs are finite; a program needn't handle non-finite values.
Results may differ from a plain program's by a relative error of at most 0.0003.
Values sent between devices are 32-bit elements; how exact they have to be, the bound alone decides.
No kernel may reach another device: no remote copies, remote signals or barrier semaphores. Data moves between devices by JAX's collectives and lax.ppermute only.
A program may use at most 64 MiB of HBM per device.

v0:
```python
import jax
import jax.numpy as jnp
from jax import lax
from jax.sharding import Mesh
from jax.sharding import PartitionSpec as P

RA_DEC = ("ra_0", "ra_1", "ra_2", "dec_0", "dec_1")
RA = ("ra_0", "ra_1", "ra_2")
DEC = ("dec_0", "dec_1")


def extended_2(cells, sides, width):
    for axis, dim in sides:
        count = lax.axis_size(axis)
        head = lax.slice_in_dim(cells, 0, width, axis=dim)
        tail = lax.slice_in_dim(cells, cells.shape[dim] - width, cells.shape[dim], axis=dim)
        cells = jnp.concatenate(
            [
                lax.ppermute(tail, axis, [(i, (i + 1) % count) for i in range(count)]),
                cells,
                lax.ppermute(head, axis, [((i + 1) % count, i) for i in range(count)]),
            ],
            axis=dim,
        )
    return cells


def over_axes(value, axes):
    for axis in axes:
        value = lax.psum(value, axis)
    return value


def pair_list():
    pairs = []
    for first in range(5):
        for second in range(first, 5):
            pairs.append((first, second))
    return pairs


def code_sums(design, observed, masked_weight, codes, windows):
    source = windows[0][:, None]
    for code in range(1, 9):
        source = jnp.where((codes == code)[None], windows[code][:, None], source)
    resid = observed
    for comp in range(5):
        resid = resid - design[comp] * source[comp]
    weighted = masked_weight * resid
    products = []
    for comp in range(5):
        products.append(design[comp] * weighted)
    for first, second in pair_list():
        products.append(masked_weight * design[first] * design[second])
    binned = []
    for code in range(9):
        hit = codes == code
        binned.append(
            jnp.stack([jnp.sum(jnp.where(hit, prod, 0.0), axis=0) for prod in products], axis=0)
        )
    return (binned, jnp.sum(weighted * resid))


def solve_blocks(stacked):
    rhs = [stacked[comp] for comp in range(5)]
    normal = [[None] * 5 for item in range(5)]
    for place, pair in enumerate(pair_list()):
        first, second = pair
        value = stacked[5 + place]
        if first == second:
            value = value + 1.0
        normal[first][second] = value
        normal[second][first] = value
    lower = [[None] * 5 for item in range(5)]
    for first in range(5):
        for second in range(first + 1):
            running = normal[first][second]
            for inner in range(second):
                running = running - lower[first][inner] * lower[second][inner]
            if first == second:
                lower[first][first] = jnp.sqrt(running)
            else:
                lower[first][second] = running / lower[second][second]
    forward = []
    for first in range(5):
        running = rhs[first]
        for inner in range(first):
            running = running - lower[first][inner] * forward[inner]
        forward.append(running / lower[first][first])
    answer = [None] * 5
    for first in range(4, -1, -1):
        running = forward[first]
        for inner in range(first + 1, 5):
            running = running - lower[inner][first] * answer[inner]
        answer[first] = running / lower[first][first]
    return jnp.stack(answer, axis=0)


def per_device(design, observed, weight, params, offsets, counts):
    cells_ra = params.shape[1]
    cells_dec = params.shape[2]
    slots = lax.broadcasted_iota(jnp.int32, observed.shape, 0)
    codes = jnp.where(slots < counts[None], offsets, 9)
    floats = jnp.concatenate([design, observed[None], weight[None]], axis=0)
    extended, extended_codes = (
        extended_2(floats, ((RA, 2), (DEC, 3)), 1),
        extended_2(codes[None], ((RA, 2), (DEC, 3)), 1),
    )
    ext_codes = extended_codes[0]
    padded_local = jnp.pad(params, ((0, 0), (2, 2), (2, 2)))
    windows = []
    for code in range(9):
        step_ra = code // 3 - 1
        step_dec = code % 3 - 1
        windows.append(
            padded_local[
                :, 1 + step_ra : 3 + step_ra + cells_ra, 1 + step_dec : 3 + step_dec + cells_dec
            ]
        )
    step_ra_all = ext_codes // 3 - 1
    step_dec_all = ext_codes % 3 - 1
    place_ra = lax.broadcasted_iota(jnp.int32, ext_codes.shape, 1) - 1 + step_ra_all
    place_dec = lax.broadcasted_iota(jnp.int32, ext_codes.shape, 2) - 1 + step_dec_all
    owned = (
        (place_ra >= 0)
        & (place_ra < cells_ra)
        & (place_dec >= 0)
        & (place_dec < cells_dec)
        & (ext_codes < 9)
    )
    masked_weight = jnp.where(owned, extended[6], jnp.zeros_like(extended[6]))
    binned, chi = code_sums(extended[:5], extended[5], masked_weight, ext_codes, windows)
    total = jnp.zeros((20, cells_ra, cells_dec), jnp.float32)
    for code in range(9):
        step_ra = code // 3 - 1
        step_dec = code % 3 - 1
        total = (
            total
            + binned[code][
                :, 1 - step_ra : 1 - step_ra + cells_ra, 1 - step_dec : 1 - step_dec + cells_dec
            ]
        )
    live_count = jnp.sum(counts).astype(jnp.float32)
    chi_total, count_total = (over_axes(chi, RA_DEC), over_axes(live_count, RA_DEC))
    new_params = params + solve_blocks(total)
    return (new_params, chi_total / count_total)


def solution(mesh):
    finer = Mesh(mesh.devices.reshape(2, 4, 2, 8, 2), ("ra_0", "ra_1", "ra_2", "dec_0", "dec_1"))
    return jax.shard_map(
        per_device,
        mesh=finer,
        in_specs=(
            P(None, None, RA, DEC),
            P(None, RA, DEC),
            P(None, RA, DEC),
            P(None, RA, DEC),
            P(None, RA, DEC),
            P(RA, DEC),
        ),
        out_specs=(P(None, RA, DEC), P()),
        check_vma=False,
    )
```

profile of v0, /device:TPU:14, one launch (start us, length us, event | category | flops | bytes accessed | tf_op | source)
XLA Modules:
  0.0 148.5 jit_solution(16316700984926354208)
XLA Ops:
  1.9 1.7 %collective-permute-start.1 = (s32[1,80,1,256]{3,1,2,0:T(8,128)S(1)}, s32[1,80,1,256]{3,1,2,0:T(8,128)S(1)}, u32[]{:S(2)}, u32[]{:S(2)}) collective-permute-start(s32[1,80,1,256]{3,1,2,0:T(8,128)S(1)} %get-tuple-element.1082), channel_id=1, source_target_pairs={{16,0},{32,16},{48,32},{64,48},{80,64},{96,80},{112,96},{128,112},... | collective-permute-start | bytes 245768 | tf_op jit(solution)/shard_map/ppermute | solution.py:21
  3.6 1.7 %copy.21 = f32[5,80,4,256]{3,1,2,0:T(8,128)S(1)} copy(f32[5,80,4,256]{3,2,1,0:T(4,128)} %param.6) | data formatting | bytes 3276800 | tf_op args[0]
  5.5 1.2 pad_maximum_fusion.4
  6.8 1.7 %collective-permute-start.5 = (f32[7,80,1,256]{3,1,2,0:T(8,128)}, f32[7,80,1,256]{3,1,2,0:T(8,128)S(1)}, u32[]{:S(2)}, u32[]{:S(2)}) collective-permute-start(f32[7,80,1,256]{3,1,2,0:T(8,128)} %get-tuple-element.1069), channel_id=1, source_target_pairs={{16,0},{32,16},{48,32},{64,48},{80,64},{96,80},{112,96},{128,112},... | collective-permute-start | bytes 1720328 | tf_op jit(solution)/shard_map/ppermute | solution.py:21
  11.2 2.2 %collective-permute-start.2 = (s32[1,80,6,1]{3,1,2,0:T(8,128)}, s32[1,80,6,1]{3,1,2,0:T(8,128)}, u32[]{:S(2)}, u32[]{:S(2)}) collective-permute-start(s32[1,80,6,1]{3,1,2,0:T(8,128)} %get-tuple-element.1077), channel_id=1, source_target_pairs={{0,1},{1,2},{2,3},{3,4},{4,5},{5,6},{6,7},{7,8},{8,9},{9,10},{10,1... | collective-permute-start | bytes 5768 | tf_op jit(solution)/shard_map/ppermute | solution.py:19
  14.7 9.9 %collective-permute-done.2 = s32[1,80,6,1]{3,1,2,0:T(8,128)} collective-permute-done((s32[1,80,6,1]{3,1,2,0:T(8,128)}, s32[1,80,6,1]{3,1,2,0:T(8,128)}, u32[]{:S(2)}, u32[]{:S(2)}) %collective-permute-start.2) | collective-permute-done | bytes 1952 | tf_op jit(solution)/shard_map/ppermute | solution.py:19
  24.6 2.2 %broadcast_compare_fusion.11 = (pred[80,6,258]{2,0,1:T(8,128)(4,1)}, s32[80,6,258]{2,0,1:T(8,128)S(1)}) fusion(s32[80,6,1]{2,0,1:T(8,128)} %bitcast.13, s32[80,6,256]{2,0,1:T(8,128)} %get-tuple-element.1079, s32[80,6,1]{2,0,1:T(8,128)} %bitcast.11), kind=kLoop, calls=%fused_computation.445 | loop fusion | flops 371520 | bytes 1114560 | tf_op jit(solution)/shard_map/eq | solution.py:45
  26.8 1.6 %broadcast_compare_fusion.10 = (pred[80,6,258]{2,0,1:T(8,128)(4,1)}, pred[80,6,258]{2,0,1:T(8,128)(4,1)}, pred[80,6,258]{2,0,1:T(8,128)(4,1)}, pred[80,6,258]{2,...) fusion(s32[80,6,258]{2,0,1:T(8,128)S(1)} %get-tuple-element.1037), kind=kLoop, calls=%fused_computation.444 | loop fusion | flops 866880 | bytes 1362240 | tf_op jit(solution)/shard_map/eq | solution.py:45
  30.3 1.8 %fusion.84 = (f32[7,80,6,1]{3,1,2,0:T(8,128)}, f32[7,80,6,1]{3,1,2,0:T(8,128)S(1)}) fusion(f32[7,80,6,256]{3,1,2,0:T(8,128)S(1)} %pad_maximum_fusion.1), kind=kLoop, calls=%fused_computation.535 | loop fusion | bytes 53760 | tf_op jit(solution)/shard_map/slice | solution.py:16
  32.1 2.6 %copy.22 = f32[7,80,6,1]{1,3,2,0:T(1,128)} copy(f32[7,80,6,1]{3,1,2,0:T(8,128)} %get-tuple-element.1066) | data formatting | bytes 26880 | tf_op jit(solution)/shard_map/slice | solution.py:16
  34.7 1.1 copy.23
  35.8 2.2 %collective-permute-start.7 = (f32[7,80,6,1]{1,3,2,0:T(1,128)}, f32[7,80,6,1]{1,3,2,0:T(1,128)}, u32[]{:S(2)}, u32[]{:S(2)}) collective-permute-start(f32[7,80,6,1]{1,3,2,0:T(1,128)} %copy.23), channel_id=1, source_target_pairs={{1,0},{2,1},{3,2},{4,3},{5,4},{6,5},{7,6},{8,7},{9,8},{10,9},{11,1... | collective-permute-start | bytes 40328 | tf_op jit(solution)/shard_map/ppermute | solution.py:21
  38.9 5.6 %select_select_fusion = f32[5,80,6,258]{3,1,2,0:T(8,128)} fusion(f32[5,6,258]{2,1,0:T(8,128)} %get-tuple-element.1094, f32[5,6,258]{2,1,0:T(8,128)} %get-tuple-element.1093, f32[5,6,258]{2,1,0:T(8,128)} %get-tuple-element.1092, f32[5,6,258]{2,1,0:T(8,128)} %get-tuple-element.1091, f32[5,6,258]{2,1,0:T(8,128)} %get-tuple-element.1090, ...), kind=kLoop, calls=%fused_computation.1 | loop fusion | flops 4953600 | bytes 3746160 | tf_op jit(solution)/shard_map/jit(_where)/select_n | solution.py:45
  45.2 1.3 copy.24
  46.5 2.5 %copy.25 = f32[7,80,6,1]{3,1,2,0:T(8,128)} copy(f32[7,80,6,1]{1,3,2,0:T(1,128)} %collective-permute-done.7) | data formatting | bytes 26880 | tf_op jit(solution)/shard_map/ppermute | solution.py:21
  49.0 5.6 %pad_maximum_fusion = f32[7,80,6,258]{3,1,2,0:T(8,128)S(1)} fusion(f32[7,80,6,1]{3,1,2,0:T(8,128)} %copy.25, f32[7,80,1,256]{3,1,2,0:T(8,128)} %copy-done.6, f32[1,80,4,256]{3,1,2,0:T(8,128)} %copy-done.1, f32[1,80,4,256]{3,1,2,0:T(8,128)} %copy-done.2, f32[5,80,4,256]{3,1,2,0:T(8,128)S(1)} %copy.21, f32[7,80,1,256]{3,1,2,0:T(8,128)} %copy-done.5, ...), kind=kLoop, calls=%fused_computation | loop fusion | flops 5201280 | bytes 6935040 | tf_op jit(solution)/shard_map/concatenate | solution.py:17
  54.6 3.3 %multiply_reduce_fusion = (f32[]{:T(128)}, f32[80,6,258]{2,0,1:T(8,128)S(1)}, f32[80,6,258]{2,0,1:T(8,128)S(1)}, s32[1,80,6,258]{3,1,2,0:T(8,128)S(1)}) fusion(f32[7,80,6,258]{3,1,2,0:T(8,128)S(1)} %pad_maximum_fusion, s32[258]{0:T(512)S(1)} %iota_add_fusion, s32[6]{0:T(128)S(1)} %iota_add_fusion.1, s32[1,80,6,1]{3,1,2,0:T(8,128)} %collective-permute-done.3, ...), kind=kLoop, calls=%fused_computation.37 | loop fusion | flops 5325119 | bytes 7926820 | tf_op jit(solution)/shard_map/reduce_sum | solution.py:61
  59.4 15.2 %select_reduce_fusion.169 = (f32[6,258]{1,0:T(8,128)S(1)}, f32[6,258]{1,0:T(8,128)S(1)}, f32[6,258]{1,0:T(8,128)S(1)}, f32[6,258]{1,0:T(8,128)S(1)}, f32[6,258]{...) fusion(f32[80,6,258]{2,0,1:T(8,128)S(1)} %get-tuple-element.105, ...), kind=kLoop, calls=%fused_computation.207 | loop fusion | flops 23266440 | bytes 7120800 | tf_op jit(solution)/shard_map/reduce_sum | solution.py:59
  74.6 14.1 %select_reduce_fusion.179 = (f32[6,258]{1,0:T(8,128)S(1)}, f32[6,258]{1,0:T(8,128)S(1)}, f32[6,258]{1,0:T(8,128)S(1)}, f32[6,258]{1,0:T(8,128)S(1)}, f32[6,258]{...) fusion(f32[80,6,258]{2,0,1:T(8,128)S(1)} %get-tuple-element.106, ...), kind=kLoop, calls=%fused_computation.217 | loop fusion | flops 22151880 | bytes 6625440 | tf_op jit(solution)/shard_map/reduce_sum | solution.py:59
  91.9 7.1 %all-reduce.5 = (f32[]{:T(128)}, f32[]{:T(128)}) all-reduce(f32[]{:T(128)} %get-tuple-element.1002, f32[]{:T(128)S(6)} %convert_element_type.5), channel_id=1, replica_groups=mesh['ra_0'=2,'ra_1'=4,'ra_2'=2,'dec_0'=8,'dec_1'=2] {'ra_0'}, use_global_device_ids=true, to_apply=%region_181.182 | all-reduce | flops 2 | bytes 16 | tf_op jit(solution)/shard_map/psum | solution.py:30
  99.0 17.4 %all-reduce.2 = (f32[]{:T(128)}, f32[]{:T(128)}) all-reduce(f32[]{:T(128)} %get-tuple-element.1000, f32[]{:T(128)} %get-tuple-element.1001), channel_id=1, replica_groups=mesh['ra_0'=2,'ra_1'=4,'ra_2'=2,'dec_0'=8,'dec_1'=2] {'ra_1'}, use_global_device_ids=true, to_apply=%region_182.183 | all-reduce | flops 2 | bytes 16 | tf_op jit(solution)/shard_map/psum | solution.py:30
  116.4 3.1 %all-reduce.4 = (f32[]{:T(128)}, f32[]{:T(128)}) all-reduce(f32[]{:T(128)} %get-tuple-element.994, f32[]{:T(128)} %get-tuple-element.995), channel_id=1, replica_groups=mesh['ra_0'=2,'ra_1'=4,'ra_2'=2,'dec_0'=8,'dec_1'=2] {'ra_2'}, use_global_device_ids=true, to_apply=%region_183.184 | all-reduce | flops 2 | bytes 16 | tf_op jit(solution)/shard_map/psum | solution.py:30
  119.5 21.1 %all-reduce.1 = (f32[]{:T(128)}, f32[]{:T(128)}) all-reduce(f32[]{:T(128)} %get-tuple-element.998, f32[]{:T(128)} %get-tuple-element.999), channel_id=1, replica_groups=mesh['ra_0'=2,'ra_1'=4,'ra_2'=2,'dec_0'=8,'dec_1'=2] {'dec_0'}, use_global_device_ids=true, to_apply=%region_184.185 | all-reduce | flops 2 | bytes 16 | tf_op jit(solution)/shard_map/psum | solution.py:30
  140.6 5.5 %all-reduce.3 = (f32[]{:T(128)}, f32[]{:T(128)}) all-reduce(f32[]{:T(128)} %get-tuple-element.992, f32[]{:T(128)} %get-tuple-element.993), channel_id=1, replica_groups=mesh['ra_0'=2,'ra_1'=4,'ra_2'=2,'dec_0'=8,'dec_1'=2] {'dec_1'}, use_global_device_ids=true, to_apply=%region_185.186 | all-reduce | flops 2 | bytes 16 | tf_op jit(solution)/shard_map/psum | solution.py:30
  (246 shorter events, 11.4 us)
Async XLA Ops:
  0.6 4.7 %copy-start.12 = (f32[80,4,256]{2,1,0:T(4,128)S(1)}, f32[80,4,256]{2,1,0:T(4,128)}, u32[]{:S(2)}) copy-start(f32[80,4,256]{2,1,0:T(4,128)} %param.8) | copy-start | bytes 983044
  0.6 4.7 %copy-start.13 = (f32[80,4,256]{2,1,0:T(4,128)S(1)}, f32[80,4,256]{2,1,0:T(4,128)}, u32[]{:S(2)}) copy-start(f32[80,4,256]{2,1,0:T(4,128)} %param.7) | copy-start | bytes 983044
  1.8 7.7 %copy-start.3 = (s32[1,80,4,256]{3,1,2,0:T(8,128)}, s32[1,80,4,256]{3,1,2,0:T(8,128)S(1)}, u32[]{:S(2)}) copy-start(s32[1,80,4,256]{3,1,2,0:T(8,128)S(1)} %fusion.38) | copy-start | bytes 983044
  1.8 7.6 %collective-permute-start = (s32[1,80,1,256]{3,1,2,0:T(8,128)S(1)}, s32[1,80,1,256]{3,1,2,0:T(8,128)S(1)}, u32[]{:S(2)}, u32[]{:S(2)}) collective-permute-start(s32[1,80,1,256]{3,1,2,0:T(8,128)S(1)} %get-tuple-element.1081), channel_id=1, source_target_pairs={{0,16},{16,32},{32,48},{48,64},{64,80},{80,96},{96,112},{112,128},... | collective-permute-start | bytes 245768 | tf_op jit(solution)/shard_map/ppermute | solution.py:19
  1.9 6.6 %copy-start.14 = (f32[5,4,256]{2,1,0:T(4,128)S(1)}, f32[5,4,256]{2,1,0:T(4,128)}, u32[]{:S(2)}) copy-start(f32[5,4,256]{2,1,0:T(4,128)} %param.9) | copy-start | bytes 61444
  1.9 7.6 %collective-permute-start.1 = (s32[1,80,1,256]{3,1,2,0:T(8,128)S(1)}, s32[1,80,1,256]{3,1,2,0:T(8,128)S(1)}, u32[]{:S(2)}, u32[]{:S(2)}) collective-permute-start(s32[1,80,1,256]{3,1,2,0:T(8,128)S(1)} %get-tuple-element.1082), channel_id=1, source_target_pairs={{16,0},{32,16},{48,32},{64,48},{80,64},{96,80},{112,96},{128,112},... | collective-permute-start | bytes 245768 | tf_op jit(solution)/shard_map/ppermute | solution.py:21
  5.4 8.0 %copy-start.16 = (s32[4,256]{1,0:T(4,128)S(1)}, s32[4,256]{1,0:T(4,128)}, u32[]{:S(2)}) copy-start(s32[4,256]{1,0:T(4,128)} %param.11) | copy-start | bytes 12292
  5.5 22.9 %copy-start.1 = (f32[1,80,4,256]{3,1,2,0:T(8,128)}, f32[1,80,4,256]{3,1,2,0:T(8,128)S(1)}, u32[]{:S(2)}) copy-start(f32[1,80,4,256]{3,1,2,0:T(8,128)S(1)} %get-tuple-element.1095) | copy-start | bytes 983044
  5.5 22.9 %copy-start.2 = (f32[1,80,4,256]{3,1,2,0:T(8,128)}, f32[1,80,4,256]{3,1,2,0:T(8,128)S(1)}, u32[]{:S(2)}) copy-start(f32[1,80,4,256]{3,1,2,0:T(8,128)S(1)} %get-tuple-element.1096) | copy-start | bytes 983044
  6.8 21.6 %collective-permute-start.4 = (f32[7,80,1,256]{3,1,2,0:T(8,128)}, f32[7,80,1,256]{3,1,2,0:T(8,128)S(1)}, u32[]{:S(2)}, u32[]{:S(2)}) collective-permute-start(f32[7,80,1,256]{3,1,2,0:T(8,128)} %get-tuple-element.1068), channel_id=1, source_target_pairs={{0,16},{16,32},{32,48},{48,64},{64,80},{80,96},{96,112},{112,128},... | collective-permute-start | bytes 1720328 | tf_op jit(solution)/shard_map/ppermute | solution.py:19
  6.8 21.6 %collective-permute-start.5 = (f32[7,80,1,256]{3,1,2,0:T(8,128)}, f32[7,80,1,256]{3,1,2,0:T(8,128)S(1)}, u32[]{:S(2)}, u32[]{:S(2)}) collective-permute-start(f32[7,80,1,256]{3,1,2,0:T(8,128)} %get-tuple-element.1069), channel_id=1, source_target_pairs={{16,0},{32,16},{48,32},{64,48},{80,64},{96,80},{112,96},{128,112},... | collective-permute-start | bytes 1720328 | tf_op jit(solution)/shard_map/ppermute | solution.py:21
  9.4 1.8 %copy-start.8 = (s32[1,80,1,256]{3,1,2,0:T(8,128)}, s32[1,80,1,256]{3,1,2,0:T(8,128)S(1)}, u32[]{:S(2)}) copy-start(s32[1,80,1,256]{3,1,2,0:T(8,128)S(1)} %collective-permute-done) | copy-start | bytes 245764
  9.5 1.7 %copy-start.10 = (s32[1,80,1,256]{3,1,2,0:T(8,128)}, s32[1,80,1,256]{3,1,2,0:T(8,128)S(1)}, u32[]{:S(2)}) copy-start(s32[1,80,1,256]{3,1,2,0:T(8,128)S(1)} %collective-permute-done.1) | copy-start | bytes 245764
  11.2 13.4 %collective-permute-start.2 = (s32[1,80,6,1]{3,1,2,0:T(8,128)}, s32[1,80,6,1]{3,1,2,0:T(8,128)}, u32[]{:S(2)}, u32[]{:S(2)}) collective-permute-start(s32[1,80,6,1]{3,1,2,0:T(8,128)} %get-tuple-element.1077), channel_id=1, source_target_pairs={{0,1},{1,2},{2,3},{3,4},{4,5},{5,6},{6,7},{7,8},{8,9},{9,10},{10,1... | collective-permute-start | bytes 5768 | tf_op jit(solution)/shard_map/ppermute | solution.py:19
  13.4 11.2 %collective-permute-start.3 = (s32[1,80,6,1]{3,1,2,0:T(8,128)}, s32[1,80,6,1]{3,1,2,0:T(8,128)}, u32[]{:S(2)}, u32[]{:S(2)}) collective-permute-start(s32[1,80,6,1]{3,1,2,0:T(8,128)} %get-tuple-element.1078), channel_id=1, source_target_pairs={{1,0},{2,1},{3,2},{4,3},{5,4},{6,5},{7,6},{8,7},{9,8},{10,9},{11,1... | collective-permute-start | bytes 5768 | tf_op jit(solution)/shard_map/ppermute | solution.py:21
  28.4 0.9 copy-start.5
  30.3 8.6 %copy-start.7 = (pred[80,6,258]{2,0,1:T(8,128)(4,1)S(1)}, pred[80,6,258]{2,0,1:T(8,128)(4,1)}, u32[]{:S(2)}) copy-start(pred[80,6,258]{2,0,1:T(8,128)(4,1)} %get-tuple-element.1036) | copy-start | bytes 371524
  35.8 10.7 %collective-permute-start.7 = (f32[7,80,6,1]{1,3,2,0:T(1,128)}, f32[7,80,6,1]{1,3,2,0:T(1,128)}, u32[]{:S(2)}, u32[]{:S(2)}) collective-permute-start(f32[7,80,6,1]{1,3,2,0:T(1,128)} %copy.23), channel_id=1, source_target_pairs={{1,0},{2,1},{3,2},{4,3},{5,4},{6,5},{7,6},{8,7},{9,8},{10,9},{11,1... | collective-permute-start | bytes 40328 | tf_op jit(solution)/shard_map/ppermute | solution.py:21
  38.0 7.2 %collective-permute-start.6 = (f32[7,80,6,1]{1,3,2,0:T(1,128)}, f32[7,80,6,1]{1,3,2,0:T(1,128)}, u32[]{:S(2)}, u32[]{:S(2)}) collective-permute-start(f32[7,80,6,1]{1,3,2,0:T(1,128)} %copy.22), channel_id=1, source_target_pairs={{0,1},{1,2},{2,3},{3,4},{4,5},{5,6},{6,7},{7,8},{8,9},{9,10},{10,1... | collective-permute-start | bytes 40328 | tf_op jit(solution)/shard_map/ppermute | solution.py:19
  49.0 5.6 %copy-start = (f32[5,80,6,258]{3,1,2,0:T(8,128)S(1)}, f32[5,80,6,258]{3,1,2,0:T(8,128)}, u32[]{:S(2)}) copy-start(f32[5,80,6,258]{3,1,2,0:T(8,128)} %select_select_fusion) | copy-start | bytes 7430404
  49.0 5.6 %copy-start.4 = (s32[1,80,4,256]{3,1,2,0:T(8,128)S(1)}, s32[1,80,4,256]{3,1,2,0:T(8,128)}, u32[]{:S(2)}) copy-start(s32[1,80,4,256]{3,1,2,0:T(8,128)} %copy-done.3) | copy-start | bytes 983044
  49.0 5.6 %copy-start.9 = (s32[1,80,1,256]{3,1,2,0:T(8,128)S(1)}, s32[1,80,1,256]{3,1,2,0:T(8,128)}, u32[]{:S(2)}) copy-start(s32[1,80,1,256]{3,1,2,0:T(8,128)} %copy-done.8) | copy-start | bytes 245764
  49.0 5.6 %copy-start.11 = (s32[1,80,1,256]{3,1,2,0:T(8,128)S(1)}, s32[1,80,1,256]{3,1,2,0:T(8,128)}, u32[]{:S(2)}) copy-start(s32[1,80,1,256]{3,1,2,0:T(8,128)} %copy-done.10) | copy-start | bytes 245764
  88.7 2.6 %copy-start.15 = (f32[5,4,256]{2,1,0:T(4,128)S(1)}, f32[5,4,256]{2,1,0:T(4,128)}, u32[]{:S(2)}) copy-start(f32[5,4,256]{2,1,0:T(4,128)} %param.9) | copy-start | bytes 61444
  (1 other events, 0.8 us)
where the time goes:
time: 149 us
  blocking collectives  54.2 us (36%)
  other arithmetic  54.1 us (36%)
  local copies, waits for them, and re-layouts  15.4 us (10%)
  waiting for transfers between devices  10.6 us (7%)
  starting transfers between devices  8.82 us (6%)
  between operations  5.4 us (4%)
    psum x5, blocking collectives, over_axes(): value = lax.psum(value, axis)  54.2 us
    reduce_sum x2, other arithmetic, code_sums(): jnp.sum(jnp.where(hit, prod, 0.0), axis=0)  29.3 us
    ppermute x4, waiting for transfers between devices, extended_2(): lax.ppermute(tail, axis, [(i, (i + 1) % count) for i in range(count)])  10.6 us
    concatenate x3, other arithmetic, extended_2(): jnp.concatenate([lax.ppermute(tail, axis, [(i, (i + 1) % count) for i in...  6.65 us
    ppermute x4, starting transfers between devices, extended_2(): lax.ppermute(head, axis, [((i + 1) % count, i) for i in range(count)])  5.65 us
    select_n x1, other arithmetic, code_sums(): source = jnp.where((codes == code)[None], windows[code][:, None], source)  5.64 us
    slice x4, local copies, waits for them, and re-layouts, extended_2(): lax.slice_in_dim(cells, cells.shape[dim] - width, cells.shape[dim], axis=...  5.24 us
    unnamed x209, local copies, waits for them, and re-layouts  4.1 us
  transfers between devices with their start and end apart: 8, of which 2 were waited for; matrix products, arithmetic and copies ran while one was open for 11% of the time, Pallas kernels for 0%

commit v1 on v0

--- a/solution.py
+++ b/solution.py
@@ -27,7 +27,8 @@
 
 def over_axes(value, axes):
     for axis in axes:
-        value = lax.psum(value, axis)
+        terms = lax.all_gather(value, axis, axis=0, tiled=False)
+        value = terms.sum(axis=0)
     return value
 
 

time: 149 us -> 213 us (1.43)
  local copies, waits for them, and re-layouts: 15.4 us -> 79.4 us
  other arithmetic: 54.1 us -> 61.5 us
  waiting for transfers between devices: 10.6 us -> 6.74 us
  blocking collectives: 54.2 us -> 50.9 us
    unnamed x209 -> x244, local copies, waits for them, and re-layouts: 4.1 us -> 65.7 us
    psum x5 -> x0, blocking collectives: 54.2 us -> none  [over_axes(): value = lax.psum(value, axis)]
    unnamed x0 -> x5, blocking collectives: none -> 50.9 us
    reduce_sum x0 -> x10, other arithmetic: none -> 6.09 us  [over_axes(): value = terms.sum(axis=0)]
    ppermute x4, waiting for transfers between devices: 10.6 us -> 6.73 us  [extended_2(): lax.ppermute(tail, axis, [(i, (i + 1) % count) for i in range(count)])]
    another operation x9, local copies, waits for them, and re-layouts: 0.03 us -> 2.41 us  [code_sums(): jnp.stack([jnp.sum(jnp.where(hit, prod, 0.0), axis=0) for prod in product...]
  transfers between devices with their start and end apart: 8 -> 8, of which waited for: 2 -> 2; matrix products, arithmetic and copies ran while one was open for 11% -> 10% of each run, Pallas kernels for 0% -> 0%
where the time goes in v1:
time: 213 us; the launch traced here: 212 us
  local copies, waits for them, and re-layouts  79.4 us (37%)
  other arithmetic  61.5 us (29%)
  blocking collectives  50.9 us (24%)
  starting transfers between devices  8.82 us (4%)
  waiting for transfers between devices  6.74 us (3%)
  between operations  4.96 us (2%)
    unnamed x244, local copies, waits for them, and re-layouts  65.7 us
    unnamed x5, blocking collectives  50.9 us
    reduce_sum x2, other arithmetic, code_sums(): jnp.sum(jnp.where(hit, prod, 0.0), axis=0)  29.3 us
    ppermute x4, waiting for transfers between devices, extended_2(): lax.ppermute(tail, axis, [(i, (i + 1) % count) for i in range(count)])  6.73 us
    concatenate x3, other arithmetic, extended_2(): jnp.concatenate([lax.ppermute(tail, axis, [(i, (i + 1) % count) for i in...  6.65 us
    reduce_sum x10, other arithmetic, over_axes(): value = terms.sum(axis=0)  6.09 us
    ppermute x4, starting transfers between devices, extended_2(): lax.ppermute(head, axis, [((i + 1) % count, i) for i in range(count)])  5.65 us
    select_n x1, other arithmetic, code_sums(): source = jnp.where((codes == code)[None], windows[code][:, None], source)  5.64 us
  transfers between devices with their start and end apart: 8, of which 2 were waited for; matrix products, arithmetic and copies ran while one was open for 10% of the time, Pallas kernels for 0%

profile of v1, /device:TPU:14, one launch (start us, length us, event | category | flops | bytes accessed | tf_op | source)
XLA Modules:
  0.0 212.3 jit_solution(17299374893881362682)
XLA Ops:
  1.9 1.7 collective-permute-start.1
  3.6 1.7 copy.21
  6.8 1.7 collective-permute-start.5
  11.3 2.2 %collective-permute-start.2 = (s32[1,80,6,1]{3,1,2,0:T(8,128)}, s32[1,80,6,1]{3,1,2,0:T(8,128)}, u32[]{:S(2)}, u32[]{:S(2)}) collective-permute-start(s32[1,80,6,1]{3,1,2,0:T(8,128)} %get-tuple-element.1077), channel_id=1, source_target_pairs={{0,1},{1,2},{2,3},{3,4},{4,5},{5,6},{6,7},{7,8},{8,9},{9,10},{10,1... | collective-permute-start | bytes 5768 | tf_op jit(solution)/shard_map/ppermute | solution.py:19
  18.6 6.0 %collective-permute-done.2 = s32[1,80,6,1]{3,1,2,0:T(8,128)} collective-permute-done((s32[1,80,6,1]{3,1,2,0:T(8,128)}, s32[1,80,6,1]{3,1,2,0:T(8,128)}, u32[]{:S(2)}, u32[]{:S(2)}) %collective-permute-start.2) | collective-permute-done | bytes 1952 | tf_op jit(solution)/shard_map/ppermute | solution.py:19
  24.7 2.2 %broadcast_compare_fusion.11 = (pred[80,6,258]{2,0,1:T(8,128)(4,1)}, s32[80,6,258]{2,0,1:T(8,128)S(1)}) fusion(s32[80,6,1]{2,0,1:T(8,128)} %bitcast.13, s32[80,6,256]{2,0,1:T(8,128)} %get-tuple-element.1079, s32[80,6,1]{2,0,1:T(8,128)} %bitcast.11), kind=kLoop, calls=%fused_computation.445 | loop fusion | flops 371520 | bytes 1114560 | tf_op jit(solution)/shard_map/eq | solution.py:46
  26.9 1.6 broadcast_compare_fusion.10
  30.4 1.8 fusion.84
  32.1 2.6 %copy.22 = f32[7,80,6,1]{1,3,2,0:T(1,128)} copy(f32[7,80,6,1]{3,1,2,0:T(8,128)} %get-tuple-element.1066) | data formatting | bytes 26880 | tf_op jit(solution)/shard_map/slice | solution.py:16
  35.9 2.2 %collective-permute-start.7 = (f32[7,80,6,1]{1,3,2,0:T(1,128)}, f32[7,80,6,1]{1,3,2,0:T(1,128)}, u32[]{:S(2)}, u32[]{:S(2)}) collective-permute-start(f32[7,80,6,1]{1,3,2,0:T(1,128)} %copy.23), channel_id=1, source_target_pairs={{1,0},{2,1},{3,2},{4,3},{5,4},{6,5},{7,6},{8,7},{9,8},{10,9},{11,1... | collective-permute-start | bytes 40328 | tf_op jit(solution)/shard_map/ppermute | solution.py:21
  39.0 5.6 %select_select_fusion = f32[5,80,6,258]{3,1,2,0:T(8,128)} fusion(f32[5,6,258]{2,1,0:T(8,128)} %get-tuple-element.1094, f32[5,6,258]{2,1,0:T(8,128)} %get-tuple-element.1093, f32[5,6,258]{2,1,0:T(8,128)} %get-tuple-element.1092, f32[5,6,258]{2,1,0:T(8,128)} %get-tuple-element.1091, f32[5,6,258]{2,1,0:T(8,128)} %get-tuple-element.1090, ...), kind=kLoop, calls=%fused_computation.1 | loop fusion | flops 4953600 | bytes 3746160 | tf_op jit(solution)/shard_map/jit(_where)/select_n | solution.py:46
  46.6 2.5 %copy.25 = f32[7,80,6,1]{3,1,2,0:T(8,128)} copy(f32[7,80,6,1]{1,3,2,0:T(1,128)} %collective-permute-done.7) | data formatting | bytes 26880 | tf_op jit(solution)/shard_map/ppermute | solution.py:21
  49.1 5.6 %pad_maximum_fusion = f32[7,80,6,258]{3,1,2,0:T(8,128)S(1)} fusion(f32[7,80,6,1]{3,1,2,0:T(8,128)} %copy.25, f32[7,80,1,256]{3,1,2,0:T(8,128)} %copy-done.6, f32[1,80,4,256]{3,1,2,0:T(8,128)} %copy-done.1, f32[1,80,4,256]{3,1,2,0:T(8,128)} %copy-done.2, f32[5,80,4,256]{3,1,2,0:T(8,128)S(1)} %copy.21, f32[7,80,1,256]{3,1,2,0:T(8,128)} %copy-done.5, ...), kind=kLoop, calls=%fused_computation | loop fusion | flops 5201280 | bytes 6935040 | tf_op jit(solution)/shard_map/concatenate | solution.py:17
  54.7 3.3 %multiply_reduce_fusion = (f32[]{:T(128)}, f32[80,6,258]{2,0,1:T(8,128)S(1)}, f32[80,6,258]{2,0,1:T(8,128)S(1)}, s32[1,80,6,258]{3,1,2,0:T(8,128)S(1)}) fusion(f32[7,80,6,258]{3,1,2,0:T(8,128)S(1)} %pad_maximum_fusion, s32[258]{0:T(512)S(1)} %iota_add_fusion, s32[6]{0:T(128)S(1)} %iota_add_fusion.1, s32[1,80,6,1]{3,1,2,0:T(8,128)} %collective-permute-done.3, ...), kind=kLoop, calls=%fused_computation.37 | loop fusion | flops 5325119 | bytes 7926820 | tf_op jit(solution)/shard_map/reduce_sum | solution.py:62
  59.4 15.2 %select_reduce_fusion.169 = (f32[6,258]{1,0:T(8,128)S(1)}, f32[6,258]{1,0:T(8,128)S(1)}, f32[6,258]{1,0:T(8,128)S(1)}, f32[6,258]{1,0:T(8,128)S(1)}, f32[6,258]{...) fusion(f32[80,6,258]{2,0,1:T(8,128)S(1)} %get-tuple-element.105, ...), kind=kLoop, calls=%fused_computation.207 | loop fusion | flops 23266440 | bytes 7120800 | tf_op jit(solution)/shard_map/reduce_sum | solution.py:60
  74.6 14.1 %select_reduce_fusion.179 = (f32[6,258]{1,0:T(8,128)S(1)}, f32[6,258]{1,0:T(8,128)S(1)}, f32[6,258]{1,0:T(8,128)S(1)}, f32[6,258]{1,0:T(8,128)S(1)}, f32[6,258]{...) fusion(f32[80,6,258]{2,0,1:T(8,128)S(1)} %get-tuple-element.106, ...), kind=kLoop, calls=%fused_computation.217 | loop fusion | flops 22151880 | bytes 6625440 | tf_op jit(solution)/shard_map/reduce_sum | solution.py:60
  91.1 1.5 dynamic-update-slice
  92.7 6.4 %all-reduce.15 = (f32[2]{0:T(128)S(1)}, f32[2]{0:T(128)S(1)}) all-reduce(f32[2]{0:T(128)S(1)} %dynamic-update-slice, f32[2]{0:T(128)S(1)} %dynamic-update-slice.5), channel_id=1, replica_groups=mesh['ra_0'=2,'ra_1'=4,'ra_2'=2,'dec_0'=8,'dec_1'=2] {'ra_0'}, use_global_device_ids=true, to_apply=%add.1 | all-reduce | flops 4 | bytes 32
  101.8 1.4 dynamic-update-slice.1
  103.3 16.7 %all-reduce.12 = (f32[4]{0:T(128)S(1)}, f32[4]{0:T(128)S(1)}) all-reduce(f32[4]{0:T(128)S(1)} %dynamic-update-slice.1, f32[4]{0:T(128)S(1)} %dynamic-update-slice.6), channel_id=1, replica_groups=mesh['ra_0'=2,'ra_1'=4,'ra_2'=2,'dec_0'=8,'dec_1'=2] {'ra_1'}, use_global_device_ids=true, to_apply=%add.2 | all-reduce | flops 8 | bytes 64
  123.9 2.4 %all-reduce.14 = (f32[2]{0:T(128)S(1)}, f32[2]{0:T(128)S(1)}) all-reduce(f32[2]{0:T(128)S(1)} %dynamic-update-slice.2, f32[2]{0:T(128)S(1)} %dynamic-update-slice.7), channel_id=1, replica_groups=mesh['ra_0'=2,'ra_1'=4,'ra_2'=2,'dec_0'=8,'dec_1'=2] {'ra_2'}, use_global_device_ids=true, to_apply=%add.3 | all-reduce | flops 4 | bytes 32
  176.8 1.6 slice_add_fusion
  178.4 20.4 %all-reduce.11 = (f32[8]{0:T(128)S(1)}, f32[8]{0:T(128)S(1)}) all-reduce(f32[8]{0:T(128)S(1)} %dynamic-update-slice.3, f32[8]{0:T(128)S(1)} %dynamic-update-slice.8), channel_id=1, replica_groups=mesh['ra_0'=2,'ra_1'=4,'ra_2'=2,'dec_0'=8,'dec_1'=2] {'dec_0'}, use_global_device_ids=true, to_apply=%add.4 | all-reduce | flops 16 | bytes 128
  203.6 4.9 %all-reduce.13 = (f32[2]{0:T(128)S(1)}, f32[2]{0:T(128)S(1)}) all-reduce(f32[2]{0:T(128)S(1)} %dynamic-update-slice.4, f32[2]{0:T(128)S(1)} %dynamic-update-slice.9), channel_id=1, replica_groups=mesh['ra_0'=2,'ra_1'=4,'ra_2'=2,'dec_0'=8,'dec_1'=2] {'dec_1'}, use_global_device_ids=true, to_apply=%add.5 | all-reduce | flops 4 | bytes 32
  (291 shorter events, 81.8 us)
Async XLA Ops:
  1.8 7.8 %copy-start.3 = (s32[1,80,4,256]{3,1,2,0:T(8,128)}, s32[1,80,4,256]{3,1,2,0:T(8,128)S(1)}, u32[]{:S(2)}) copy-start(s32[1,80,4,256]{3,1,2,0:T(8,128)S(1)} %fusion.38) | copy-start | bytes 983044
  1.8 7.7 %collective-permute-start = (s32[1,80,1,256]{3,1,2,0:T(8,128)S(1)}, s32[1,80,1,256]{3,1,2,0:T(8,128)S(1)}, u32[]{:S(2)}, u32[]{:S(2)}) collective-permute-start(s32[1,80,1,256]{3,1,2,0:T(8,128)S(1)} %get-tuple-element.1081), channel_id=1, source_target_pairs={{0,16},{16,32},{32,48},{48,64},{64,80},{80,96},{96,112},{112,128},... | collective-permute-start | bytes 245768 | tf_op jit(solution)/shard_map/ppermute | solution.py:19
  1.9 6.7 %copy-start.14 = (f32[5,4,256]{2,1,0:T(4,128)S(1)}, f32[5,4,256]{2,1,0:T(4,128)}, u32[]{:S(2)}) copy-start(f32[5,4,256]{2,1,0:T(4,128)} %param.9) | copy-start | bytes 61444
  1.9 7.6 %collective-permute-start.1 = (s32[1,80,1,256]{3,1,2,0:T(8,128)S(1)}, s32[1,80,1,256]{3,1,2,0:T(8,128)S(1)}, u32[]{:S(2)}, u32[]{:S(2)}) collective-permute-start(s32[1,80,1,256]{3,1,2,0:T(8,128)S(1)} %get-tuple-element.1082), channel_id=1, source_target_pairs={{16,0},{32,16},{48,32},{64,48},{80,64},{96,80},{112,96},{128,112},... | collective-permute-start | bytes 245768 | tf_op jit(solution)/shard_map/ppermute | solution.py:21
  5.4 8.1 %copy-start.16 = (s32[4,256]{1,0:T(4,128)S(1)}, s32[4,256]{1,0:T(4,128)}, u32[]{:S(2)}) copy-start(s32[4,256]{1,0:T(4,128)} %param.11) | copy-start | bytes 12292
  5.4 9.4 %copy-start.21 = (u32[256]{0:T(256)S(1)}, u32[256]{0:T(256)}, u32[]{:S(2)}) copy-start(u32[256]{0:T(256)} %constant.81) | copy-start | bytes 3076
  5.4 10.0 %copy-start.20 = (u32[256]{0:T(256)S(1)}, u32[256]{0:T(256)}, u32[]{:S(2)}) copy-start(u32[256]{0:T(256)} %constant.76) | copy-start | bytes 3076
  5.4 10.5 %copy-start.19 = (u32[256]{0:T(256)S(1)}, u32[256]{0:T(256)}, u32[]{:S(2)}) copy-start(u32[256]{0:T(256)} %constant.71) | copy-start | bytes 3076
  5.4 11.2 %copy-start.18 = (u32[256]{0:T(256)S(1)}, u32[256]{0:T(256)}, u32[]{:S(2)}) copy-start(u32[256]{0:T(256)} %constant.66) | copy-start | bytes 3076
  5.4 11.8 %copy-start.17 = (u32[256]{0:T(256)S(1)}, u32[256]{0:T(256)}, u32[]{:S(2)}) copy-start(u32[256]{0:T(256)} %constant.61) | copy-start | bytes 3076
  5.6 22.9 %copy-start.1 = (f32[1,80,4,256]{3,1,2,0:T(8,128)}, f32[1,80,4,256]{3,1,2,0:T(8,128)S(1)}, u32[]{:S(2)}) copy-start(f32[1,80,4,256]{3,1,2,0:T(8,128)S(1)} %get-tuple-element.1095) | copy-start | bytes 983044
  5.6 22.9 %copy-start.2 = (f32[1,80,4,256]{3,1,2,0:T(8,128)}, f32[1,80,4,256]{3,1,2,0:T(8,128)S(1)}, u32[]{:S(2)}) copy-start(f32[1,80,4,256]{3,1,2,0:T(8,128)S(1)} %get-tuple-element.1096) | copy-start | bytes 983044
  6.8 21.6 %collective-permute-start.4 = (f32[7,80,1,256]{3,1,2,0:T(8,128)}, f32[7,80,1,256]{3,1,2,0:T(8,128)S(1)}, u32[]{:S(2)}, u32[]{:S(2)}) collective-permute-start(f32[7,80,1,256]{3,1,2,0:T(8,128)} %get-tuple-element.1068), channel_id=1, source_target_pairs={{0,16},{16,32},{32,48},{48,64},{64,80},{80,96},{96,112},{112,128},... | collective-permute-start | bytes 1720328 | tf_op jit(solution)/shard_map/ppermute | solution.py:19
  6.8 21.6 %collective-permute-start.5 = (f32[7,80,1,256]{3,1,2,0:T(8,128)}, f32[7,80,1,256]{3,1,2,0:T(8,128)S(1)}, u32[]{:S(2)}, u32[]{:S(2)}) collective-permute-start(f32[7,80,1,256]{3,1,2,0:T(8,128)} %get-tuple-element.1069), channel_id=1, source_target_pairs={{16,0},{32,16},{48,32},{64,48},{80,64},{96,80},{112,96},{128,112},... | collective-permute-start | bytes 1720328 | tf_op jit(solution)/shard_map/ppermute | solution.py:21
  11.3 13.4 %collective-permute-start.2 = (s32[1,80,6,1]{3,1,2,0:T(8,128)}, s32[1,80,6,1]{3,1,2,0:T(8,128)}, u32[]{:S(2)}, u32[]{:S(2)}) collective-permute-start(s32[1,80,6,1]{3,1,2,0:T(8,128)} %get-tuple-element.1077), channel_id=1, source_target_pairs={{0,1},{1,2},{2,3},{3,4},{4,5},{5,6},{6,7},{7,8},{8,9},{9,10},{10,1... | collective-permute-start | bytes 5768 | tf_op jit(solution)/shard_map/ppermute | solution.py:19
  13.4 11.2 %collective-permute-start.3 = (s32[1,80,6,1]{3,1,2,0:T(8,128)}, s32[1,80,6,1]{3,1,2,0:T(8,128)}, u32[]{:S(2)}, u32[]{:S(2)}) collective-permute-start(s32[1,80,6,1]{3,1,2,0:T(8,128)} %get-tuple-element.1078), channel_id=1, source_target_pairs={{1,0},{2,1},{3,2},{4,3},{5,4},{6,5},{7,6},{8,7},{9,8},{10,9},{11,1... | collective-permute-start | bytes 5768 | tf_op jit(solution)/shard_map/ppermute | solution.py:21
  30.4 8.6 %copy-start.7 = (pred[80,6,258]{2,0,1:T(8,128)(4,1)S(1)}, pred[80,6,258]{2,0,1:T(8,128)(4,1)}, u32[]{:S(2)}) copy-start(pred[80,6,258]{2,0,1:T(8,128)(4,1)} %get-tuple-element.1036) | copy-start | bytes 371524
  35.9 10.7 %collective-permute-start.7 = (f32[7,80,6,1]{1,3,2,0:T(1,128)}, f32[7,80,6,1]{1,3,2,0:T(1,128)}, u32[]{:S(2)}, u32[]{:S(2)}) collective-permute-start(f32[7,80,6,1]{1,3,2,0:T(1,128)} %copy.23), channel_id=1, source_target_pairs={{1,0},{2,1},{3,2},{4,3},{5,4},{6,5},{7,6},{8,7},{9,8},{10,9},{11,1... | collective-permute-start | bytes 40328 | tf_op jit(solution)/shard_map/ppermute | solution.py:21
  38.1 7.2 %collective-permute-start.6 = (f32[7,80,6,1]{1,3,2,0:T(1,128)}, f32[7,80,6,1]{1,3,2,0:T(1,128)}, u32[]{:S(2)}, u32[]{:S(2)}) collective-permute-start(f32[7,80,6,1]{1,3,2,0:T(1,128)} %copy.22), channel_id=1, source_target_pairs={{0,1},{1,2},{2,3},{3,4},{4,5},{5,6},{6,7},{7,8},{8,9},{9,10},{10,1... | collective-permute-start | bytes 40328 | tf_op jit(solution)/shard_map/ppermute | solution.py:19
  49.1 5.6 %copy-start = (f32[5,80,6,258]{3,1,2,0:T(8,128)S(1)}, f32[5,80,6,258]{3,1,2,0:T(8,128)}, u32[]{:S(2)}) copy-start(f32[5,80,6,258]{3,1,2,0:T(8,128)} %select_select_fusion) | copy-start | bytes 7430404
  49.1 5.6 %copy-start.4 = (s32[1,80,4,256]{3,1,2,0:T(8,128)S(1)}, s32[1,80,4,256]{3,1,2,0:T(8,128)}, u32[]{:S(2)}) copy-start(s32[1,80,4,256]{3,1,2,0:T(8,128)} %copy-done.3) | copy-start | bytes 983044
  49.1 5.6 %copy-start.9 = (s32[1,80,1,256]{3,1,2,0:T(8,128)S(1)}, s32[1,80,1,256]{3,1,2,0:T(8,128)}, u32[]{:S(2)}) copy-start(s32[1,80,1,256]{3,1,2,0:T(8,128)} %copy-done.8) | copy-start | bytes 245764
  49.1 5.6 %copy-start.11 = (s32[1,80,1,256]{3,1,2,0:T(8,128)S(1)}, s32[1,80,1,256]{3,1,2,0:T(8,128)}, u32[]{:S(2)}) copy-start(s32[1,80,1,256]{3,1,2,0:T(8,128)} %copy-done.10) | copy-start | bytes 245764
  88.7 114.2 %copy-start.15 = (f32[5,4,256]{2,1,0:T(4,128)S(1)}, f32[5,4,256]{2,1,0:T(4,128)}, u32[]{:S(2)}) copy-start(f32[5,4,256]{2,1,0:T(4,128)} %param.9) | copy-start | bytes 61444
  (6 other events, 14.6 us)
